TPU v7x, 32 devices: a whole 2x2x4 slice. The times are simulated.
32 devices in a mesh: fsdp: 4 (over z), tp: 8 (over y, x, core).
Axes of the slice: x: 2, y: 2, z: 4, core: 2. Of those that a mesh axis runs over, the one named last changes fastest.
Arguments:
- tokens: bfloat16 [3008, 4096], P('fsdp', 'tp'), may hold values from -6 to 6
- norm_gain: float32 [4096], replicated, may hold values from 0.5 to 1.5
- base_gate: bfloat16 [4096, 12288], P(None, 'tp'), may hold values from -0.09375 to 0.09375
- base_up: bfloat16 [4096, 12288], P(None, 'tp'), may hold values from -0.09375 to 0.09375
- base_down: bfloat16 [12288, 4096], P('tp'), may hold values from -0.0546875 to 0.0546875
- code_gate: bfloat16 [4096, 12288], P(('fsdp', 'tp')), may hold values from -4 to 4
- code_up: bfloat16 [4096, 12288], P(('fsdp', 'tp')), may hold values from -4 to 4
- scale_gate: float32 [4096, 96], P(('fsdp', 'tp')), may hold values from 0.005 to 0.05
- scale_up: float32 [4096, 96], P(('fsdp', 'tp')), may hold values from 0.005 to 0.05
- code_down: bfloat16 [12288, 4096], P(None, ('fsdp', 'tp')), may hold values from -4 to 4
- scale_down: float32 [96, 4096], P(None, ('fsdp', 'tp')), may hold values from 0.005 to 0.05
- cu_seqlens: int32 [4, 9], P('fsdp'), may hold values from 0 to 752, as said below
Outputs:
- mixed: bfloat16 [3008, 4096], P('fsdp', 'tp')
- seq_means: float32 [32, 4096], P('fsdp', 'tp')
Inputs may be any that keep to these rules, and one draw needn't show every extreme that they name: `cu_seqlens`: each row starts at 0 and rises strictly; its last entry is the group's live tokens, which fill the first slots of its 752. Over all groups the live tokens add up to exactly 1536, and some group has exactly 752.
All inputs are finite; a program needn't handle non-finite values.
Results may differ from a plain program's by a relative error of at most 0.023.
Values may be sent and summed in bfloat16 or wider, within the bound.
A program may use at most 256 MiB of HBM per device.

v0:
```python
import jax
import jax.numpy as jnp
from jax import lax
from jax.sharding import PartitionSpec as P

SEQS = 8


EPSILON = 1e-06


def dequant_rows(base_part, code_part, scales):
    height, breadth = code_part.shape
    blocks = scales.shape[1]
    spread_out = (
        code_part.astype(jnp.float32).reshape(height, blocks, breadth // blocks)
        * scales[:, :, None]
    )
    return (base_part.astype(jnp.float32) + spread_out.reshape(height, breadth)).astype(
        jnp.bfloat16
    )


def dequant_cols(base_part, code_part, scales):
    height, breadth = code_part.shape
    blocks = scales.shape[0]
    spread_out = (
        code_part.astype(jnp.float32).reshape(blocks, height // blocks, breadth)
        * scales[:, None, :]
    )
    return (base_part.astype(jnp.float32) + spread_out.reshape(height, breadth)).astype(
        jnp.bfloat16
    )


def forward(
    rows_in,
    norm_gain,
    base_gate,
    base_up,
    base_down,
    code_gate,
    code_up,
    scale_gate,
    scale_up,
    code_down,
    scale_down,
):
    gathered = lax.all_gather(rows_in, "tp", axis=1, tiled=True)
    widened = gathered.astype(jnp.float32)
    inverse = lax.rsqrt(jnp.mean(widened * widened, axis=1, keepdims=True) + EPSILON)
    normed = (widened * inverse * norm_gain[None, :]).astype(jnp.bfloat16)
    sliced = (
        lax.all_to_all(code_gate, "tp", split_axis=1, concat_axis=0, tiled=True),
        lax.all_to_all(code_up, "tp", split_axis=1, concat_axis=0, tiled=True),
        lax.all_to_all(
            scale_gate.astype(jnp.bfloat16), "tp", split_axis=1, concat_axis=0, tiled=True
        ).astype(scale_gate.dtype),
        lax.all_to_all(
            scale_up.astype(jnp.bfloat16), "tp", split_axis=1, concat_axis=0, tiled=True
        ).astype(scale_up.dtype),
    )
    pieces = (
        lax.all_gather(sliced[0], "fsdp", axis=0, tiled=True),
        lax.all_gather(sliced[1], "fsdp", axis=0, tiled=True),
        lax.all_gather(sliced[2].astype(jnp.bfloat16), "fsdp", axis=0, tiled=True).astype(
            jnp.float32
        ),
        lax.all_gather(sliced[3].astype(jnp.bfloat16), "fsdp", axis=0, tiled=True).astype(
            jnp.float32
        ),
    )
    gate_add = jnp.dot(
        normed, dequant_rows(base_gate, pieces[0], pieces[2]), preferred_element_type=jnp.float32
    )
    up_add = jnp.dot(
        normed, dequant_rows(base_up, pieces[1], pieces[3]), preferred_element_type=jnp.float32
    )
    hidden = (jax.nn.silu(gate_add) * up_add).astype(jnp.bfloat16)
    sliced_down = (
        lax.all_to_all(code_down, "tp", split_axis=0, concat_axis=1, tiled=True),
        lax.all_to_all(
            scale_down.astype(jnp.bfloat16), "tp", split_axis=0, concat_axis=1, tiled=True
        ).astype(scale_down.dtype),
    )
    pieces = (
        lax.all_gather(sliced_down[0], "fsdp", axis=1, tiled=True),
        lax.all_gather(sliced_down[1].astype(jnp.bfloat16), "fsdp", axis=1, tiled=True).astype(
            jnp.float32
        ),
    )
    block_out = jnp.dot(
        hidden, dequant_cols(base_down, pieces[0], pieces[1]), preferred_element_type=jnp.float32
    )
    summed = lax.psum_scatter(
        block_out.astype(jnp.bfloat16), "tp", scatter_dimension=1, tiled=True
    ).astype(jnp.float32)
    return (rows_in.astype(jnp.float32) + summed).astype(jnp.bfloat16)


def shards(
    tokens,
    norm_gain,
    base_gate,
    base_up,
    base_down,
    code_gate,
    code_up,
    scale_gate,
    scale_up,
    code_down,
    scale_down,
    cu_seqlens,
):
    capacity = tokens.shape[0]
    bounds = cu_seqlens[0]
    live_count = bounds[SEQS]
    positions = jnp.arange(capacity, dtype=jnp.int32)
    mixed_rows = forward(
        tokens,
        norm_gain,
        base_gate,
        base_up,
        base_down,
        code_gate,
        code_up,
        scale_gate,
        scale_up,
        code_down,
        scale_down,
    )
    mixed_rows = jnp.where(
        (positions < live_count)[:, None], mixed_rows, jnp.zeros((), jnp.bfloat16)
    )
    member = (positions[None, :] >= bounds[:-1, None]) & (positions[None, :] < bounds[1:, None])
    seq_sums = jnp.dot(member.astype(jnp.bfloat16), mixed_rows, preferred_element_type=jnp.float32)
    lengths = (bounds[1:] - bounds[:-1]).astype(jnp.float32)
    return (mixed_rows, seq_sums / lengths[:, None])


def solution(mesh):
    placed = (
        P("fsdp", "tp"),
        P(),
        P(None, "tp"),
        P(None, "tp"),
        P("tp", None),
        P(("fsdp", "tp"), None),
        P(("fsdp", "tp"), None),
        P(("fsdp", "tp"), None),
        P(("fsdp", "tp"), None),
        P(None, ("fsdp", "tp")),
        P(None, ("fsdp", "tp")),
        P("fsdp", None),
    )
    return jax.shard_map(
        shards,
        mesh=mesh,
        in_specs=placed,
        out_specs=(P("fsdp", "tp"), P("fsdp", "tp")),
        check_vma=False,
    )
```

profile of v0, /device:TPU:0, one launch (start us, length us, event | category | flops | bytes accessed | tf_op | source)
XLA Modules:
  0.0 834.5 jit_solution(9441921378246151597)
XLA Ops:
  7.2 0.0 all-gather.5.cloned.1.call-start
  7.2 0.7 all-gather.5.cloned.1.call-update
  7.9 0.0 all-gather.7.cloned.1.call-start
  7.9 3.5 copy.26
  11.4 57.3 %all_to_all.114 = bf16[128,8,1536]{0,2,1:T(8,128)(2,1)S(1)} all-to-all(bf16[128,8,1536]{0,2,1:T(8,128)(2,1)S(1)} %bitcast.81), channel_id=1, replica_groups=mesh['fsdp'=4,'tp'=8] {'tp'}, dimensions={1} | all-to-all | bytes 6291456 | tf_op jit(solution)/shard_map/all_to_all | solution.py:54
  68.8 2.1 copy_bitcast_fusion.2
  70.9 0.0 all-gather.7.cloned.1.call-update
  70.9 0.0 all-gather.9.cloned.1.call-start
  71.0 3.5 copy.30
  74.4 40.3 %all_to_all.115 = bf16[128,8,1536]{0,2,1:T(8,128)(2,1)S(1)} all-to-all(bf16[128,8,1536]{0,2,1:T(8,128)(2,1)S(1)} %bitcast.82), channel_id=1, replica_groups=mesh['fsdp'=4,'tp'=8] {'tp'}, dimensions={1} | all-to-all | bytes 6291456 | tf_op jit(solution)/shard_map/all_to_all | solution.py:55
  114.7 2.1 copy_bitcast_fusion.1
  116.9 0.0 all-gather.9.cloned.1.call-update
  116.9 0.0 all-gather.11.cloned.1.call-start
  116.9 41.4 %all_to_all.116 = bf16[8,1536,128]{2,1,0:T(8,128)(2,1)S(1)} all-to-all(bf16[8,1536,128]{2,1,0:T(8,128)(2,1)} %bitcast.83), channel_id=1, replica_groups=mesh['fsdp'=4,'tp'=8] {'tp'}, dimensions={0} | all-to-all | bytes 6291456 | tf_op jit(solution)/shard_map/all_to_all | solution.py:81
  158.3 2.2 copy_bitcast_fusion
  160.5 0.0 all-gather.11.cloned.1.call-update
  160.5 0.6 all_to_all.88
  161.1 3.3 all-to-all-start.1
  164.5 16.8 %copy.25 = bf16[4096,1536]{0,1:T(8,128)(2,1)} copy(bf16[4096,1536]{1,0:T(8,128)(2,1)} %param.14) | data formatting | bytes 25165824 | tf_op args[2]
  181.3 16.1 %copy.29 = bf16[4096,1536]{0,1:T(8,128)(2,1)} copy(bf16[4096,1536]{1,0:T(8,128)(2,1)} %param.15) | data formatting | bytes 25165824 | tf_op args[3]
  197.4 0.6 all_to_all.96
  198.0 0.6 all_to_all.104
  198.6 4.2 all-to-all-start.3
  202.9 22.0 %all_gather.23 = bf16[4096,12]{0,1:T(8,128)(2,1)S(1)} all-gather(bf16[1024,12]{0,1:T(8,128)(2,1)S(1)} %bitcast.84), channel_id=1, replica_groups=mesh['fsdp'=4,'tp'=8] {'fsdp'}, dimensions={0}, use_global_device_ids=true | all-gather | bytes 122880 | tf_op jit(solution)/shard_map/all_gather | solution.py:66
  224.9 4.0 all-to-all-start.5
  228.9 0.0 reduce-scatter.2.cloned.1.call-start
  229.0 26.2 %all_gather.25 = bf16[4096,12]{0,1:T(8,128)(2,1)S(1)} all-gather(bf16[1024,12]{0,1:T(8,128)(2,1)S(1)} %bitcast.85), channel_id=1, replica_groups=mesh['fsdp'=4,'tp'=8] {'fsdp'}, dimensions={0}, use_global_device_ids=true | all-gather | bytes 122880 | tf_op jit(solution)/shard_map/all_gather | solution.py:69
  255.3 19.9 %all_gather.27 = bf16[12,4096]{1,0:T(8,128)(2,1)S(1)} all-gather(bf16[12,1024]{1,0:T(8,128)(2,1)S(1)} %bitcast.86), channel_id=1, replica_groups=mesh['fsdp'=4,'tp'=8] {'fsdp'}, dimensions={1}, use_global_device_ids=true | all-gather | bytes 122880 | tf_op jit(solution)/shard_map/all_gather | solution.py:88
  275.2 0.0 all-gather.5.cloned.1.call-done
  275.3 4.0 fusion.6
  279.3 28.5 %all-gather.7.cloned.1.call-done = bf16[4096,1536]{0,1:T(8,128)(2,1)} async-done(((bf16[1024,1536]{0,1:T(8,128)(2,1)}), bf16[4096,1536]{0,1:T(8,128)(2,1)}) %all-gather.7.cloned.1.call-update) | async-done | bytes 12582928 | tf_op jit(solution)/shard_map/all_gather | solution.py:64
  307.8 16.4 %fusion.5 = bf16[4096,1536]{0,1:T(8,128)(2,1)} fusion(bf16[4096,1536]{0,1:T(8,128)(2,1)} %all-gather.7.cloned.1.call-done, bf16[4096,1536]{0,1:T(8,128)(2,1)} %copy.25, f32[4096,12]{0,1:T(8,128)S(1)} %convert_element_type.86), kind=kLoop, calls=%fused_computation.8 | loop fusion | flops 31457280 | bytes 37945344 | tf_op jit(solution)/shard_map/convert_element_type | solution.py:19
  324.2 201.6 %all-gather.9.cloned.1.call-done = bf16[4096,1536]{0,1:T(8,128)(2,1)} async-done(((bf16[1024,1536]{0,1:T(8,128)(2,1)}), bf16[4096,1536]{0,1:T(8,128)(2,1)}) %all-gather.9.cloned.1.call-update) | async-done | bytes 12582928 | tf_op jit(solution)/shard_map/all_gather | solution.py:65
  525.8 16.8 %fusion.3 = bf16[4096,1536]{0,1:T(8,128)(2,1)} fusion(bf16[4096,1536]{0,1:T(8,128)(2,1)} %all-gather.9.cloned.1.call-done, bf16[4096,1536]{0,1:T(8,128)(2,1)} %copy.29, f32[4096,12]{0,1:T(8,128)S(1)} %convert_element_type.91), kind=kLoop, calls=%fused_computation.5 | loop fusion | flops 31457280 | bytes 37945344 | tf_op jit(solution)/shard_map/convert_element_type | solution.py:19
  542.6 1.7 copy-done
  544.3 13.5 %fusion.12 = f32[752,1536]{1,0:T(8,128)} fusion(bf16[4096,1536]{0,1:T(8,128)(2,1)S(1)} %copy-done, bf16[752,4096]{1,0:T(8,128)(2,1)} %all-gather.5.cloned.1.call-done, f32[4096]{0:T(1024)S(1)} %copy-done.7, f32[752]{0:T(1024)S(1)} %add_rsqrt_fusion), kind=kOutput, calls=%fused_computation.20 | convolution fusion | flops 9474670592 | bytes 23382976 | tf_op jit(solution)/shard_map/dot_general | solution.py:73
  557.8 16.7 %multiply_convert_fusion.clone.4 = bf16[752,1536]{1,0:T(8,128)(2,1)} fusion(f32[752,1536]{1,0:T(8,128)} %fusion.12, bf16[4096,1536]{0,1:T(8,128)(2,1)} %fusion.3, bf16[752,4096]{1,0:T(8,128)(2,1)} %all-gather.5.cloned.1.call-done, f32[4096]{0:T(1024)S(1)} %copy-done.7, f32[752]{0:T(1024)S(1)} %add_rsqrt_fusion), kind=kOutput, calls=%fused_computation.15.clone.clone.clone.1 | convolution fusion | flops 9481601024 | bytes 25693120 | tf_op jit(solution)/shard_map/dot_general | solution.py:76
  574.5 169.1 %all-gather.11.cloned.1.call-done = bf16[1536,4096]{1,0:T(8,128)(2,1)} async-done(((bf16[1536,1024]{1,0:T(8,128)(2,1)}), bf16[1536,4096]{1,0:T(8,128)(2,1)}) %all-gather.11.cloned.1.call-update) | async-done | bytes 12582928 | tf_op jit(solution)/shard_map/all_gather | solution.py:87
  743.6 11.4 %fusion.1 = bf16[1536,4096]{1,0:T(8,128)(2,1)S(1)} fusion(bf16[1536,4096]{1,0:T(8,128)(2,1)} %all-gather.11.cloned.1.call-done, bf16[1536,4096]{1,0:T(8,128)(2,1)} %param.16, f32[12,4096]{1,0:T(8,128)S(1)} %convert_element_type.97), kind=kLoop, calls=%fused_computation.2 | loop fusion | flops 31457280 | bytes 37945344 | tf_op jit(solution)/shard_map/convert_element_type | solution.py:31
  755.1 11.5 %convolution_convert_fusion = bf16[752,4096]{1,0:T(8,128)(2,1)} fusion(bf16[1536,4096]{1,0:T(8,128)(2,1)S(1)} %fusion.1, bf16[752,1536]{1,0:T(8,128)(2,1)S(1)} %copy-done.8), kind=kOutput, calls=%fused_computation.14 | convolution fusion | flops 9465430016 | bytes 21053440 | tf_op jit(solution)/shard_map/dot_general | solution.py:92
  766.6 0.0 reduce-scatter.2.cloned.1.call-update
  766.6 0.6 slice.14
  767.2 0.6 iota_compare_fusion.3
  767.8 0.1 subtract_convert_fusion
  767.9 0.1 slice_bitcast_fusion.1
  768.0 57.7 %reduce-scatter.2.cloned.1.call-done = bf16[752,512]{1,0:T(8,128)(2,1)} async-done(((bf16[752,4096]{1,0:T(8,128)(2,1)}), bf16[752,512]{1,0:T(8,128)(2,1)}) %reduce-scatter.2.cloned.1.call-update) | async-done | bytes 770064 | tf_op jit(solution)/shard_map/reduce_scatter | solution.py:95
  825.7 1.4 fusion.14
  827.1 0.9 convolution_divide_fusion
  (36 shorter events, 0.2 us)
Async XLA Ops:
  7.2 268.1 %all-gather.5.cloned.1.call-start = ((), (), s32[]{:S(2)}) async-start(), calls=%async_computation.7 | async-start | bytes 6930432 | tf_op jit(solution)/shard_map/all_gather | solution.py:49
  7.9 299.9 %all-gather.7.cloned.1.call-start = ((), (), s32[]{:S(2)}) async-start(), calls=%async_computation.8 | async-start | bytes 15728640 | tf_op jit(solution)/shard_map/all_gather | solution.py:64
  70.9 454.9 %all-gather.9.cloned.1.call-start = ((), (), s32[]{:S(2)}) async-start(), calls=%async_computation.9 | async-start | bytes 15728640 | tf_op jit(solution)/shard_map/all_gather | solution.py:65
  114.7 45.8 %copy-start.3 = (f32[128,96]{0,1:T(8,128)S(1)}, f32[128,96]{0,1:T(8,128)}, u32[]{:S(2)}) copy-start(f32[128,96]{0,1:T(8,128)} %param.19) | copy-start | bytes 147460
  116.9 626.8 %all-gather.11.cloned.1.call-start = ((), (), s32[]{:S(2)}) async-start(), calls=%async_computation.10 | async-start | bytes 15728640 | tf_op jit(solution)/shard_map/all_gather | solution.py:87
  161.1 37.5 %all-to-all-start.1 = ((bf16[128,8,12]{0,2,1:T(8,128)(2,1)}), bf16[128,8,12]{0,2,1:T(8,128)(2,1)S(1)}, u32[]{:S(2)}, u32[]{:S(2)}) async-start(bf16[128,8,12]{0,2,1:T(8,128)(2,1)} %all_to_all.88), calls=%async_computation.1 | async-start | bytes 65536 | tf_op jit(solution)/shard_map/all_to_all | solution.py:56
  181.3 16.1 %copy-start.4 = (f32[128,96]{0,1:T(8,128)S(1)}, f32[128,96]{0,1:T(8,128)}, u32[]{:S(2)}) copy-start(f32[128,96]{0,1:T(8,128)} %param.20) | copy-start | bytes 147460
  181.3 16.7 %copy-start.5 = (f32[96,128]{1,0:T(8,128)S(1)}, f32[96,128]{1,0:T(8,128)}, u32[]{:S(2)}) copy-start(f32[96,128]{1,0:T(8,128)} %param.22) | copy-start | bytes 147460
  198.6 26.2 %all-to-all-start.3 = ((bf16[128,8,12]{0,2,1:T(8,128)(2,1)}), bf16[128,8,12]{0,2,1:T(8,128)(2,1)S(1)}, u32[]{:S(2)}, u32[]{:S(2)}) async-start(bf16[128,8,12]{0,2,1:T(8,128)(2,1)} %all_to_all.96), calls=%async_computation.3 | async-start | bytes 65536 | tf_op jit(solution)/shard_map/all_to_all | solution.py:59
  224.9 30.4 %all-to-all-start.5 = ((bf16[8,12,128]{2,1,0:T(8,128)(2,1)}), bf16[8,12,128]{2,1,0:T(8,128)(2,1)S(1)}, u32[]{:S(2)}, u32[]{:S(2)}) async-start(bf16[8,12,128]{2,1,0:T(8,128)(2,1)} %all_to_all.104), calls=%async_computation.5 | async-start | bytes 65536 | tf_op jit(solution)/shard_map/all_to_all | solution.py:82
  228.9 596.8 %reduce-scatter.2.cloned.1.call-start = ((), (), s32[]{:S(2)}) async-start(), calls=%async_computation.11 | async-start | bytes 6930432 | tf_op jit(solution)/shard_map/reduce_scatter | solution.py:95
  324.2 218.4 %copy-start.7 = (f32[4096]{0:T(1024)S(1)}, f32[4096]{0:T(1024)}, u32[]{:S(2)}) copy-start(f32[4096]{0:T(1024)} %param.13) | copy-start | bytes 49156
  525.8 18.5 %copy-start = (bf16[4096,1536]{0,1:T(8,128)(2,1)S(1)}, bf16[4096,1536]{0,1:T(8,128)(2,1)}, u32[]{:S(2)}) copy-start(bf16[4096,1536]{0,1:T(8,128)(2,1)} %fusion.5) | copy-start | bytes 37748740
  743.6 11.4 %copy-start.8 = (bf16[752,1536]{1,0:T(8,128)(2,1)S(1)}, bf16[752,1536]{1,0:T(8,128)(2,1)}, u32[]{:S(2)}) copy-start(bf16[752,1536]{1,0:T(8,128)(2,1)} %multiply_convert_fusion.clone.4) | copy-start | bytes 6930436
  755.0 11.6 %copy-start.6 = (s32[1,9]{1,0:T(1,128)S(1)}, s32[1,9]{1,0:T(1,128)}, u32[]{:S(2)}) copy-start(s32[1,9]{1,0:T(1,128)} %param.23) | copy-start | bytes 112
  755.1 70.7 %copy-start.1 = (bf16[752,512]{1,0:T(8,128)(2,1)S(1)}, bf16[752,512]{1,0:T(8,128)(2,1)}, u32[]{:S(2)}) copy-start(bf16[752,512]{1,0:T(8,128)(2,1)} %param.12) | copy-start | bytes 2310148
  827.1 0.9 copy-start.2
Sparse Core Ops, SparseCore 0:
  9.8 71.2 all-gather.4
  82.7 225.0 all-gather.6
  309.4 216.4 all-gather.8
  527.2 216.3 all-gather.10
  766.7 58.9 reduce-scatter.1
where the time goes:
time: 836 us; the launch traced here: 835 us
  waiting for transfers between devices  458 us (55%)
  blocking collectives  207 us (25%)
  other arithmetic  50.8 us (6%)
  local copies, waits for them, and re-layouts  50.6 us (6%)
  matrix products  42.6 us (5%)
  between operations  14 us (2%)
  starting transfers between devices  11.7 us (1%)
    all_gather x1, waiting for transfers between devices, forward(): lax.all_gather(sliced[1], 'fsdp', axis=0, tiled=True)  202 us
    all_gather x1, waiting for transfers between devices, forward(): lax.all_gather(sliced_down[0], 'fsdp', axis=1, tiled=True)  169 us
    reduce_scatter x1, waiting for transfers between devices, forward(): lax.psum_scatter(block_out.astype(jnp.bfloat16), 'tp', scatter_dimension=...  57.7 us
    all_to_all x1, blocking collectives, forward(): lax.all_to_all(code_gate, 'tp', split_axis=1, concat_axis=0, tiled=True)  57.3 us
    unnamed x28, local copies, waits for them, and re-layouts  41.6 us
    all_to_all x1, blocking collectives, forward(): lax.all_to_all(code_down, 'tp', split_axis=0, concat_axis=1, tiled=True)  41.4 us
    all_to_all x1, blocking collectives, forward(): lax.all_to_all(code_up, 'tp', split_axis=1, concat_axis=0, tiled=True)  40.3 us
    convert_element_type x2, other arithmetic, dequant_rows(): (base_part.astype(jnp.float32) + spread_out.reshape(height, breadth)).ast...  33.3 us
  transfers between devices with their start and end apart: 8, of which 4 were waited for; matrix products, arithmetic and copies ran while one was open for 14% of the time, Pallas kernels for 0%

commit v1 on v0

v1 whole, which is shorter than its diff:
```python
import jax
import jax.numpy as jnp
from jax import lax
from jax.sharding import PartitionSpec as P

SEQS = 8
EPSILON = 1e-06
F32, BF16 = jnp.float32, jnp.bfloat16


def dequant_rows(base_part, code_part, scales):
    rows, cols = code_part.shape
    blocks = scales.shape[1]
    delta = code_part.astype(F32).reshape(rows, blocks, cols // blocks) * scales[:, :, None]
    return (base_part.astype(F32) + delta.reshape(rows, cols)).astype(BF16)


def dequant_cols(base_part, code_part, scales):
    rows, cols = code_part.shape
    blocks = scales.shape[0]
    delta = code_part.astype(F32).reshape(blocks, rows // blocks, cols) * scales[:, None, :]
    return (base_part.astype(F32) + delta.reshape(rows, cols)).astype(BF16)


def swap_up(part, axis_name="tp"):
    return lax.all_to_all(part, axis_name, split_axis=1, concat_axis=0, tiled=True)


def swap_down(part):
    return lax.all_to_all(part, "tp", split_axis=0, concat_axis=1, tiled=True)


def shards(tokens, norm_gain, base_gate, base_up, base_down, code_gate, code_up,
           scale_gate, scale_up, code_down, scale_down, cu_seqlens):
    groups = lax.axis_size("fsdp")
    slices = lax.axis_size("tp")
    me_f = lax.axis_index("fsdp")
    me_t = lax.axis_index("tp")
    cap, feat = tokens.shape
    width = base_gate.shape[0]
    depth = width // groups
    units = base_gate.shape[1]
    live_all = groups * (cap // 2 + SEQS)
    grain = 16 * slices
    capp = -(-cap // grain) * grain
    part = capp // slices

    padded = jnp.pad(tokens, ((0, capp - cap), (0, 0)))
    rows_full = lax.all_to_all(padded, "tp", split_axis=0, concat_axis=1, tiled=True)
    wide = rows_full.astype(F32)
    inverse = lax.rsqrt(jnp.mean(wide * wide, axis=1, keepdims=True) + EPSILON)
    normed = (wide * inverse * norm_gain[None, :]).astype(BF16)
    block = swap_up(normed, "fsdp")
    every = lax.all_gather(block, "tp", axis=0, tiled=True)

    bounds_all = lax.all_gather(cu_seqlens, "fsdp", axis=0, tiled=True)
    counts = bounds_all[:, SEQS]
    ends = jnp.cumsum(counts)
    starts = ends - counts
    place = jnp.arange(live_all, dtype=jnp.int32)
    group_of = jnp.sum((place[:, None] >= ends[None, :]).astype(jnp.int32), axis=1)
    group_of = jnp.minimum(group_of, groups - 1)
    slot = place - jnp.take(starts, group_of)
    source = (slot // part) * (groups * part) + group_of * part + slot % part
    pick = (source[:, None] == jnp.arange(slices * groups * part, dtype=jnp.int32)[None, :]).astype(BF16)
    packed = jnp.dot(pick, every, preferred_element_type=F32).astype(BF16)

    gate_rows = lax.dynamic_slice_in_dim(base_gate, me_f * depth, depth, 0)
    up_rows = lax.dynamic_slice_in_dim(base_up, me_f * depth, depth, 0)
    w_gate = dequant_rows(gate_rows, swap_up(code_gate), swap_up(scale_gate))
    w_up = dequant_rows(up_rows, swap_up(code_up), swap_up(scale_up))
    partial = jnp.concatenate(
        [jnp.dot(packed, w_gate, preferred_element_type=F32).astype(BF16),
         jnp.dot(packed, w_up, preferred_element_type=F32).astype(BF16)], axis=1)
    summed = lax.psum_scatter(partial, "fsdp", scatter_dimension=0, tiled=True).astype(F32)
    hidden = (jax.nn.silu(summed[:, :units]) * summed[:, units:]).astype(BF16)
    hidden_all = lax.all_gather(hidden, "fsdp", axis=0, tiled=True)

    down_cols = lax.dynamic_slice_in_dim(base_down, me_f * depth, depth, 1)
    w_down = dequant_cols(down_cols, swap_down(code_down), swap_down(scale_down))
    out_part = jnp.dot(hidden_all, w_down, preferred_element_type=F32).astype(BF16)
    out_cols = lax.psum_scatter(out_part, "tp", scatter_dimension=1, tiled=True)
    narrow = out_cols.shape[1]

    grp = jnp.arange(groups, dtype=jnp.int32)
    slots = jnp.arange(cap, dtype=jnp.int32)
    wanted = jnp.where(slots[None, :] < counts[:, None], starts[:, None] + slots[None, :], -1)
    spread = (wanted.reshape(-1)[:, None] == place[None, :]).astype(BF16)
    placed_rows = jnp.dot(spread, out_cols, preferred_element_type=F32).astype(BF16)
    mine = lax.all_to_all(placed_rows.reshape(groups, cap, narrow), "fsdp", split_axis=0, concat_axis=0, tiled=True)
    ratio = slices // groups
    span = slices // ratio
    half = me_t // span
    pick_half = (jnp.arange(ratio) == half)[None, :, None, None]
    outgoing = jnp.where(pick_half, mine[:, None], jnp.zeros((), BF16)).reshape(slices, cap, narrow)
    incoming = lax.all_to_all(outgoing, "tp", split_axis=0, concat_axis=0, tiled=True)
    take_from = lax.dynamic_slice_in_dim(incoming, (me_t % ratio) * span, span, 0)
    summed_out = take_from.transpose(1, 0, 2).reshape(cap, feat).astype(F32)

    bounds = cu_seqlens[0]
    live_count = bounds[SEQS]
    mixed = (tokens.astype(F32) + summed_out).astype(BF16)
    mixed = jnp.where((slots < live_count)[:, None], mixed, jnp.zeros((), BF16))
    member = (slots[None, :] >= bounds[:-1, None]) & (slots[None, :] < bounds[1:, None])
    seq_sums = jnp.dot(member.astype(BF16), mixed, preferred_element_type=F32)
    lengths = (bounds[1:] - bounds[:-1]).astype(F32)
    return mixed, seq_sums / lengths[:, None]


def solution(mesh):
    placed = (
        P("fsdp", "tp"), P(), P(None, "tp"), P(None, "tp"), P("tp", None),
        P(("fsdp", "tp"), None), P(("fsdp", "tp"), None),
        P(("fsdp", "tp"), None), P(("fsdp", "tp"), None),
        P(None, ("fsdp", "tp")), P(None, ("fsdp", "tp")), P("fsdp", None),
    )
    return jax.shard_map(shards, mesh=mesh, in_specs=placed,
                         out_specs=(P("fsdp", "tp"), P("fsdp", "tp")), check_vma=False)
```

time: 836 us -> 608 us (0.73)
  blocking collectives: 207 us -> 39.8 us
  waiting for transfers between devices: 458 us -> 392 us
  starting transfers between devices: 11.7 us -> 33.6 us
  other arithmetic: 50.8 us -> 38.2 us
    all_gather x4 -> x2, waiting for transfers between devices: 399 us -> 35.9 us  [the longest x1 35.9 us: shards(): hidden_all = lax.all_gather(hidden, 'fsdp', axis=0, tiled=True)]
    unnamed x5 -> x6, waiting for transfers between devices: 0.75 us -> 203 us
    all_to_all x3 -> x8, waiting for transfers between devices: 0.01 us -> 153 us  [the longest x4 66 us: swap_up(): lax.all_to_all(part, axis_name, split_axis=1, concat_axis=0, tiled=True)]
    all_to_all x3 -> x2, blocking collectives: 139 us -> 30.6 us  [the longest x1 22.1 us: swap_up(): lax.all_to_all(part, axis_name, split_axis=1, concat_axis=0, tiled=True)]
    all_gather x3 -> x1, blocking collectives: 68.1 us -> 9.21 us  [shards(): bounds_all = lax.all_gather(cu_seqlens, 'fsdp', axis=0, tiled=True)]
    reduce_scatter x1 -> x0, waiting for transfers between devices: 57.7 us -> none  [forward(): lax.psum_scatter(block_out.astype(jnp.bfloat16), 'tp', scatter_dimension=...]
    convert_element_type x10 -> x9, other arithmetic: 44.8 us -> 19.3 us  [the longest x2 10.3 us: dequant_rows(): return (base_part.astype(F32) + delta.reshape(rows, cols)).astype(BF16)]
    all_to_all x3 -> x8, starting transfers between devices: 11.5 us -> 33.4 us  [the longest x4 16.2 us: swap_up(): lax.all_to_all(part, axis_name, split_axis=1, concat_axis=0, tiled=True)]
  transfers between devices with their start and end apart: 8 -> 12, of which waited for: 4 -> 11; matrix products, arithmetic and copies ran while one was open for 14% -> 7% of each run, Pallas kernels for 0% -> 0%
where the time goes in v1:
time: 608 us; the launch traced here: 606 us
  waiting for transfers between devices  392 us (64%)
  local copies, waits for them, and re-layouts  49.8 us (8%)
  blocking collectives  39.8 us (7%)
  matrix products  38.4 us (6%)
  other arithmetic  38.2 us (6%)
  starting transfers between devices  33.6 us (6%)
  between operations  14.2 us (2%)
    unnamed x6, waiting for transfers between devices  203 us
    all_to_all x4, waiting for transfers between devices, swap_up(): lax.all_to_all(part, axis_name, split_axis=1, concat_axis=0, tiled=True)  66 us
    all_to_all x1, waiting for transfers between devices, swap_down(): return lax.all_to_all(part, 'tp', split_axis=0, concat_axis=1, tiled=True)  37.7 us
    unnamed x35, local copies, waits for them, and re-layouts  36.4 us
    all_gather x1, waiting for transfers between devices, shards(): hidden_all = lax.all_gather(hidden, 'fsdp', axis=0, tiled=True)  35.9 us
    all_to_all x1, blocking collectives, swap_up(): lax.all_to_all(part, axis_name, split_axis=1, concat_axis=0, tiled=True)  22.1 us
    all_to_all x1, waiting for transfers between devices, shards(): lax.all_to_all(placed_rows.reshape(groups, cap, narrow), 'fsdp', split_ax...  19.5 us
    all_to_all x1, waiting for transfers between devices, shards(): lax.all_to_all(outgoing, 'tp', split_axis=0, concat_axis=0, tiled=True)  18 us
  transfers between devices with their start and end apart: 12, of which 11 were waited for; matrix products, arithmetic and copies ran while one was open for 7% of the time, Pallas kernels for 0%

profile of v1, /device:TPU:0, one launch (start us, length us, event | category | flops | bytes accessed | tf_op | source)
XLA Modules:
  0.0 605.9 jit_solution(8563752525326372813)
XLA Ops:
  7.2 2.1 pad.4
  9.3 5.2 all-to-all-start
  15.2 11.8 %all-to-all-done = bf16[8,96,512]{2,1,0:T(8,128)(2,1)S(1)} async-done(((bf16[8,96,512]{2,1,0:T(8,128)(2,1)}), bf16[8,96,512]{2,1,0:T(8,128)(2,1)S(1)}, u32[]{:S(2)}, u32[]{:S(2)}) %all-to-all-start) | async-done | bytes 786464 | tf_op jit(solution)/shard_map/all_to_all | solution.py:49
  28.1 1.9 reshape.201
  30.4 2.0 multiply_convert_fusion
  32.6 22.1 %all_to_all.126 = bf16[96,4,1024]{2,0,1:T(8,128)(2,1)} all-to-all(bf16[96,4,1024]{2,0,1:T(8,128)(2,1)S(1)} %copy.58), channel_id=1, replica_groups=mesh['fsdp'=4,'tp'=8] {'fsdp'}, dimensions={1} | all-to-all | bytes 1572864 | tf_op jit(solution)/shard_map/all_to_all | solution.py:26
  55.4 4.8 all-to-all-start.3
  60.8 4.4 all-to-all-done.3
  65.2 3.4 all-to-all-start.5
  68.6 2.9 copy.60
  71.5 2.9 all-to-all-done.5
  74.4 3.6 all-to-all-start.2
  78.1 4.9 copy.64
  83.0 49.7 %all-to-all-done.2 = bf16[128,8,1536]{0,2,1:T(8,128)(2,1)S(1)} async-done(((bf16[128,8,1536]{0,2,1:T(8,128)(2,1)}), bf16[128,8,1536]{0,2,1:T(8,128)(2,1)S(1)}, u32[]{:S(2)}, u32[]{:S(2)}) %all-to-all-start.2) | async-done | bytes 3145760 | tf_op jit(solution)/shard_map/all_to_all | solution.py:26
  132.7 1.6 copy-done
  134.3 4.5 all-to-all-start.4
  138.8 9.2 %all-gather = s32[4,1,9]{2,1,0:T(1,128)S(1)} all-gather(s32[1,1,9]{2,1,0:T(1,128)S(1)} %bitcast.124), channel_id=1, replica_groups=mesh['fsdp'=4,'tp'=8] {'fsdp'}, dimensions={0}, use_global_device_ids=true | all-gather | bytes 180 | tf_op jit(solution)/shard_map/all_gather | solution.py:56
  148.2 2.1 constant_dynamic-slice_fusion.1
  150.2 2.9 copy.75
  153.1 2.1 constant_dynamic-slice_fusion
  155.2 2.9 copy.76
  159.1 2.6 fusion.25
  161.9 5.7 fusion.9
  167.6 9.0 %all-to-all-done.4 = bf16[128,8,1536]{0,2,1:T(8,128)(2,1)} async-done(((bf16[128,8,1536]{0,2,1:T(8,128)(2,1)}), bf16[128,8,1536]{0,2,1:T(8,128)(2,1)}, u32[]{:S(2)}, u32[]{:S(2)}) %all-to-all-start.4) | async-done | bytes 3145760 | tf_op jit(solution)/shard_map/all_to_all | solution.py:26
  176.6 4.6 fusion.7
  181.2 12.7 %fusion.10 = bf16[1536,1024]{1,0:T(8,128)(2,1)S(1)} fusion(bf16[3072,1024]{1,0:T(8,128)(2,1)} %all-gather.4.cloned.1.call-done, s32[1536]{0:T(1024)S(1)} %fusion.23), kind=kOutput, calls=%fused_computation.22 | convolution fusion | flops 9669967872 | bytes 9443328 | tf_op jit(solution)/shard_map/dot_general | solution.py:66
  193.9 5.4 convolution_convert_fusion.1
  199.4 5.6 convolution_convert_fusion
  205.0 12.2 %pad_maximum_fusion = bf16[1536,3072]{0,1:T(8,128)(2,1)} fusion(bf16[1536,1536]{0,1:T(8,128)(2,1)S(1)} %convolution_convert_fusion, bf16[1536,1536]{0,1:T(8,128)(2,1)S(1)} %convolution_convert_fusion.1), kind=kLoop, calls=%fused_computation.4 | loop fusion | flops 18874368 | bytes 18874368 | tf_op jit(solution)/shard_map/concatenate | solution.py:72
  217.2 12.7 %copy.71 = bf16[1536,3072]{1,0:T(8,128)(2,1)} copy(bf16[1536,3072]{0,1:T(8,128)(2,1)} %pad_maximum_fusion) | data formatting | bytes 18874368
  230.0 158.6 %reduce-scatter.7.cloned.1.call-done = bf16[384,3072]{1,0:T(8,128)(2,1)} async-done(((bf16[1536,3072]{1,0:T(8,128)(2,1)}), bf16[384,3072]{1,0:T(8,128)(2,1)}) %reduce-scatter.7.cloned.1.call-update) | async-done | bytes 2359312
  388.6 3.0 copy.72
  391.9 1.8 fusion.12
  393.7 8.5 %all_to_all.127 = f32[8,12,128]{2,1,0:T(8,128)S(1)} all-to-all(f32[8,12,128]{2,1,0:T(8,128)S(1)} %all_to_all.111), channel_id=1, replica_groups=mesh['fsdp'=4,'tp'=8] {'tp'}, dimensions={0} | all-to-all | bytes 98304 | tf_op jit(solution)/shard_map/all_to_all | solution.py:30
  402.2 3.7 all-to-all-start.6
  406.0 37.7 %all-to-all-done.6 = bf16[8,1536,128]{2,1,0:T(8,128)(2,1)S(1)} async-done(((bf16[8,1536,128]{2,1,0:T(8,128)(2,1)}), bf16[8,1536,128]{2,1,0:T(8,128)(2,1)S(1)}, u32[]{:S(2)}, u32[]{:S(2)}) %all-to-all-start.6) | async-done | bytes 3145760 | tf_op jit(solution)/shard_map/all_to_all | solution.py:30
  443.7 4.6 fusion.5
  448.3 35.9 %all-gather.6.cloned.1.call-done = bf16[1536,1536]{0,1:T(8,128)(2,1)} async-done(((bf16[384,1536]{0,1:T(8,128)(2,1)}), bf16[1536,1536]{0,1:T(8,128)(2,1)}) %all-gather.6.cloned.1.call-update) | async-done | bytes 4718608 | tf_op jit(solution)/shard_map/all_gather | solution.py:77
  484.2 8.2 %convolution_convert_fusion.2 = bf16[1536,1024]{1,0:T(8,128)(2,1)S(1)} fusion(bf16[1536,1536]{0,1:T(8,128)(2,1)} %all-gather.6.cloned.1.call-done, bf16[1536,1024]{1,0:T(8,128)(2,1)} %fusion.5), kind=kOutput, calls=%fused_computation.21 | convolution fusion | flops 4833411072 | bytes 11010048 | tf_op jit(solution)/shard_map/dot_general | solution.py:81
  492.3 3.0 copy.73
  495.5 44.5 %reduce-scatter.9.cloned.1.call-done = bf16[128,1536]{1,0:T(8,128)(2,1)} async-done(((bf16[1024,1536]{1,0:T(8,128)(2,1)}), bf16[128,1536]{1,0:T(8,128)(2,1)}) %reduce-scatter.9.cloned.1.call-update) | async-done | bytes 393232
  540.0 5.5 fusion.11
  545.5 4.7 all-to-all-start.8
  550.4 19.5 %all-to-all-done.8 = bf16[4,752,128]{2,1,0:T(8,128)(2,1)S(1)} async-done(((bf16[4,752,128]{2,1,0:T(8,128)(2,1)}), bf16[4,752,128]{2,1,0:T(8,128)(2,1)S(1)}, u32[]{:S(2)}, u32[]{:S(2)}) %all-to-all-start.8) | async-done | bytes 770080 | tf_op jit(solution)/shard_map/all_to_all | solution.py:90
  569.8 1.3 bitcast_select_fusion
  571.2 3.6 all-to-all-start.9
  577.3 18.0 %all-to-all-done.9 = bf16[8,752,128]{2,1,0:T(8,128)(2,1)S(1)} async-done(((bf16[8,752,128]{2,1,0:T(8,128)(2,1)}), bf16[8,752,128]{2,1,0:T(8,128)(2,1)S(1)}, u32[]{:S(2)}, u32[]{:S(2)}) %all-to-all-start.9) | async-done | bytes 1540128 | tf_op jit(solution)/shard_map/all_to_all | solution.py:96
  595.9 1.4 fusion.15
  (69 shorter events, 10.8 us)
Async XLA Ops:
  9.3 17.8 %all-to-all-start = ((bf16[8,96,512]{2,1,0:T(8,128)(2,1)}), bf16[8,96,512]{2,1,0:T(8,128)(2,1)S(1)}, u32[]{:S(2)}, u32[]{:S(2)}) async-start(bf16[8,96,512]{2,1,0:T(8,128)(2,1)} %bitcast.7), calls=%async_computation | async-start | bytes 1572864 | tf_op jit(solution)/shard_map/all_to_all | solution.py:49
  14.5 166.8 %all-gather.4.cloned.1.call-start = ((), (), s32[]{:S(2)}) async-start(), calls=%async_computation.12 | async-start | bytes 7077888 | tf_op jit(solution)/shard_map/all_gather | solution.py:54
  30.3 24.4 %copy-start.6 = (f32[128,96]{0,1:T(8,128)S(1)}, f32[128,96]{0,1:T(8,128)}, u32[]{:S(2)}) copy-start(f32[128,96]{0,1:T(8,128)} %param.19) | copy-start | bytes 147460
  30.4 29.8 %copy-start.7 = (f32[128,96]{0,1:T(8,128)S(1)}, f32[128,96]{0,1:T(8,128)}, u32[]{:S(2)}) copy-start(f32[128,96]{0,1:T(8,128)} %param.20) | copy-start | bytes 147460
  30.4 38.2 %copy-start.2 = (bf16[128,12288]{1,0:T(8,128)(2,1)S(1)}, bf16[128,12288]{1,0:T(8,128)(2,1)}, u32[]{:S(2)}) copy-start(bf16[128,12288]{1,0:T(8,128)(2,1)} %param.17) | copy-start | bytes 9437188
  55.4 9.8 %all-to-all-start.3 = ((f32[128,8,12]{0,2,1:T(8,128)}), f32[128,8,12]{0,2,1:T(8,128)S(1)}, u32[]{:S(2)}, u32[]{:S(2)}) async-start(f32[128,8,12]{0,2,1:T(8,128)} %all_to_all.101), calls=%async_computation.3 | async-start | bytes 131072 | tf_op jit(solution)/shard_map/all_to_all | solution.py:26
  65.2 9.2 %all-to-all-start.5 = ((f32[128,8,12]{0,2,1:T(8,128)}), f32[128,8,12]{0,2,1:T(8,128)S(1)}, u32[]{:S(2)}, u32[]{:S(2)}) async-start(f32[128,8,12]{0,2,1:T(8,128)} %all_to_all.106), calls=%async_computation.5 | async-start | bytes 131072 | tf_op jit(solution)/shard_map/all_to_all | solution.py:26
  74.4 58.2 %all-to-all-start.2 = ((bf16[128,8,1536]{0,2,1:T(8,128)(2,1)}), bf16[128,8,1536]{0,2,1:T(8,128)(2,1)S(1)}, u32[]{:S(2)}, u32[]{:S(2)}) async-start(bf16[128,8,1536]{0,2,1:T(8,128)(2,1)} %bitcast.11), calls=%async_computation.2 | async-start | bytes 6291456 | tf_op jit(solution)/shard_map/all_to_all | solution.py:26
  132.7 1.6 copy-start
  132.7 6.2 %copy-start.9 = (s32[1,9]{1,0:T(1,128)S(1)}, s32[1,9]{1,0:T(1,128)}, u32[]{:S(2)}) copy-start(s32[1,9]{1,0:T(1,128)} %param.23) | copy-start | bytes 112
  134.3 42.3 %all-to-all-start.4 = ((bf16[128,8,1536]{0,2,1:T(8,128)(2,1)}), bf16[128,8,1536]{0,2,1:T(8,128)(2,1)}, u32[]{:S(2)}, u32[]{:S(2)}) async-start(bf16[128,8,1536]{0,2,1:T(8,128)(2,1)} %bitcast.15), calls=%async_computation.4 | async-start | bytes 6291456 | tf_op jit(solution)/shard_map/all_to_all | solution.py:26
  138.8 249.8 %reduce-scatter.7.cloned.1.call-start = ((), (), s32[]{:S(2)}) async-start(), calls=%async_computation.14 | async-start | bytes 11796480
  161.9 14.8 %copy-start.1 = (bf16[1024,1536]{0,1:T(8,128)(2,1)S(1)}, bf16[1024,1536]{0,1:T(8,128)(2,1)}, u32[]{:S(2)}) copy-start(bf16[1024,1536]{0,1:T(8,128)(2,1)} %copy.76) | copy-start | bytes 9437188
  181.2 12.7 %copy-start.3 = (bf16[1024,1536]{0,1:T(8,128)(2,1)S(1)}, bf16[1024,1536]{0,1:T(8,128)(2,1)}, u32[]{:S(2)}) copy-start(bf16[1024,1536]{0,1:T(8,128)(2,1)} %fusion.9) | copy-start | bytes 9437188
  193.9 5.4 copy-start.4
  230.0 254.2 %all-gather.6.cloned.1.call-start = ((), (), s32[]{:S(2)}) async-start(), calls=%async_computation.13 | async-start | bytes 5898240 | tf_op jit(solution)/shard_map/all_gather | solution.py:77
  391.9 1.8 copy-start.8
  402.2 41.5 %all-to-all-start.6 = ((bf16[8,1536,128]{2,1,0:T(8,128)(2,1)}), bf16[8,1536,128]{2,1,0:T(8,128)(2,1)S(1)}, u32[]{:S(2)}, u32[]{:S(2)}) async-start(bf16[8,1536,128]{2,1,0:T(8,128)(2,1)} %bitcast.109), calls=%async_computation.6 | async-start | bytes 6291456 | tf_op jit(solution)/shard_map/all_to_all | solution.py:30
  405.9 134.1 %reduce-scatter.9.cloned.1.call-start = ((), (), s32[]{:S(2)}) async-start(), calls=%async_computation.15 | async-start | bytes 3538944
  545.5 29.2 %copy-start.5 = (bf16[752,512]{1,0:T(8,128)(2,1)S(1)}, bf16[752,512]{1,0:T(8,128)(2,1)}, u32[]{:S(2)}) copy-start(bf16[752,512]{1,0:T(8,128)(2,1)} %param.12) | copy-start | bytes 2310148
  545.5 24.3 %all-to-all-start.8 = ((bf16[4,752,128]{2,1,0:T(8,128)(2,1)}), bf16[4,752,128]{2,1,0:T(8,128)(2,1)S(1)}, u32[]{:S(2)}, u32[]{:S(2)}) async-start(bf16[4,752,128]{2,1,0:T(8,128)(2,1)} %bitcast.23), calls=%async_computation.8 | async-start | bytes 1540096 | tf_op jit(solution)/shard_map/all_to_all | solution.py:90
  571.2 24.2 %all-to-all-start.9 = ((bf16[8,752,128]{2,1,0:T(8,128)(2,1)}), bf16[8,752,128]{2,1,0:T(8,128)(2,1)S(1)}, u32[]{:S(2)}, u32[]{:S(2)}) async-start(bf16[8,752,128]{2,1,0:T(8,128)(2,1)} %bitcast_select_fusion), calls=%async_computation.9 | async-start | bytes 3080192 | tf_op jit(solution)/shard_map/all_to_all | solution.py:96
Sparse Core Ops, SparseCore 0:
  54.9 70.2 all-gather.3
  230.1 158.4 reduce-scatter.6
  393.8 90.2 all-gather.5
  495.4 44.4 reduce-scatter.8

commit v2 on v1

--- a/solution.py
+++ b/solution.py
@@ -69,15 +69,19 @@
     up_rows = lax.dynamic_slice_in_dim(base_up, me_f * depth, depth, 0)
     w_gate = dequant_rows(gate_rows, swap_up(code_gate), swap_up(scale_gate))
     w_up = dequant_rows(up_rows, swap_up(code_up), swap_up(scale_up))
-    partial = jnp.concatenate(
-        [jnp.dot(packed, w_gate, preferred_element_type=F32).astype(BF16),
-         jnp.dot(packed, w_up, preferred_element_type=F32).astype(BF16)], axis=1)
-    summed = lax.psum_scatter(partial, "fsdp", scatter_dimension=0, tiled=True).astype(F32)
-    hidden = (jax.nn.silu(summed[:, :units]) * summed[:, units:]).astype(BF16)
+    gate_part = jnp.dot(packed, w_gate, preferred_element_type=F32).astype(BF16)
+    up_part = jnp.dot(packed, w_up, preferred_element_type=F32).astype(BF16)
+    up_part, code_down = lax.optimization_barrier((up_part, code_down))
+    gate_sum = lax.psum_scatter(gate_part, "fsdp", scatter_dimension=0, tiled=True)
+    up_sum = lax.psum_scatter(up_part, "fsdp", scatter_dimension=0, tiled=True)
+    down_codes, down_scales = swap_down(code_down), swap_down(scale_down)
+    gate_sum, up_sum, down_codes, down_scales = lax.optimization_barrier(
+        (gate_sum, up_sum, down_codes, down_scales))
+    hidden = (jax.nn.silu(gate_sum.astype(F32)) * up_sum.astype(F32)).astype(BF16)
     hidden_all = lax.all_gather(hidden, "fsdp", axis=0, tiled=True)
 
     down_cols = lax.dynamic_slice_in_dim(base_down, me_f * depth, depth, 1)
-    w_down = dequant_cols(down_cols, swap_down(code_down), swap_down(scale_down))
+    w_down = dequant_cols(down_cols, down_codes, down_scales)
     out_part = jnp.dot(hidden_all, w_down, preferred_element_type=F32).astype(BF16)
     out_cols = lax.psum_scatter(out_part, "tp", scatter_dimension=1, tiled=True)
     narrow = out_cols.shape[1]

time: 608 us -> 538 us (0.88)
  waiting for transfers between devices: 392 us -> 347 us
  local copies, waits for them, and re-layouts: 49.8 us -> 35.5 us
  other arithmetic: 38.2 us -> 25.4 us
    unnamed x6, waiting for transfers between devices: 203 us -> 44.5 us
    reduce_scatter x0 -> x2, waiting for transfers between devices: none -> 58.8 us  [the longest x1 58.8 us: shards(): up_sum = lax.psum_scatter(up_part, 'fsdp', scatter_dimension=0, tiled=True)]
    all_gather x1, waiting for transfers between devices: 35.9 us -> 84.9 us  [shards(): hidden_all = lax.all_gather(hidden, 'fsdp', axis=0, tiled=True)]
    unnamed x35 -> x33, local copies, waits for them, and re-layouts: 36.4 us -> 20 us
    concatenate x1 -> x0, other arithmetic: 12.2 us -> none  [shards(): jnp.concatenate([jnp.dot(packed, w_gate, preferred_element_type=F32).asty...]
  transfers between devices with their start and end apart: 12 -> 13, of which waited for: 11 -> 12; matrix products, arithmetic and copies ran while one was open for 7% -> 8% of each run, Pallas kernels for 0% -> 0%
where the time goes in v2:
time: 538 us; the launch traced here: 536 us
  waiting for transfers between devices  347 us (64%)
  matrix products  40.9 us (8%)
  blocking collectives  38.7 us (7%)
  local copies, waits for them, and re-layouts  35.5 us (7%)
  starting transfers between devices  34.8 us (6%)
  other arithmetic  25.4 us (5%)
  between operations  14.1 us (3%)
    all_gather x1, waiting for transfers between devices, shards(): hidden_all = lax.all_gather(hidden, 'fsdp', axis=0, tiled=True)  84.9 us
    all_to_all x4, waiting for transfers between devices, swap_up(): lax.all_to_all(part, axis_name, split_axis=1, concat_axis=0, tiled=True)  71.8 us
    reduce_scatter x1, waiting for transfers between devices, shards(): up_sum = lax.psum_scatter(up_part, 'fsdp', scatter_dimension=0, tiled=True)  58.8 us
    unnamed x6, waiting for transfers between devices  44.5 us
    all_to_all x1, waiting for transfers between devices, swap_down(): return lax.all_to_all(part, 'tp', split_axis=0, concat_axis=1, tiled=True)  37.7 us
    all_to_all x1, blocking collectives, swap_up(): lax.all_to_all(part, axis_name, split_axis=1, concat_axis=0, tiled=True)  22.1 us
    unnamed x33, local copies, waits for them, and re-layouts  20 us
    all_to_all x1, waiting for transfers between devices, shards(): lax.all_to_all(placed_rows.reshape(groups, cap, narrow), 'fsdp', split_ax...  19.5 us
  transfers between devices with their start and end apart: 13, of which 12 were waited for; matrix products, arithmetic and copies ran while one was open for 8% of the time, Pallas kernels for 0%

profile of v2, /device:TPU:0, one launch (start us, length us, event | category | flops | bytes accessed | tf_op | source)
XLA Modules:
  0.0 536.5 jit_solution(2134350978414402686)
XLA Ops:
  7.2 2.1 pad.4
  9.3 5.2 all-to-all-start
  15.2 11.8 %all-to-all-done = bf16[8,96,512]{2,1,0:T(8,128)(2,1)S(1)} async-done(((bf16[8,96,512]{2,1,0:T(8,128)(2,1)}), bf16[8,96,512]{2,1,0:T(8,128)(2,1)S(1)}, u32[]{:S(2)}, u32[]{:S(2)}) %all-to-all-start) | async-done | bytes 786464 | tf_op jit(solution)/shard_map/all_to_all | solution.py:49
  28.1 1.9 reshape.196
  30.4 2.0 multiply_convert_fusion
  32.6 22.1 %all_to_all.135 = bf16[96,4,1024]{2,0,1:T(8,128)(2,1)} all-to-all(bf16[96,4,1024]{2,0,1:T(8,128)(2,1)S(1)} %copy.58), channel_id=1, replica_groups=mesh['fsdp'=4,'tp'=8] {'fsdp'}, dimensions={1} | all-to-all | bytes 1572864 | tf_op jit(solution)/shard_map/all_to_all | solution.py:26
  55.4 4.8 all-to-all-start.3
  60.2 2.9 copy.60
  63.0 2.2 all-to-all-done.3
  65.2 4.6 all-to-all-start.2
  69.9 9.2 %all-gather = s32[4,1,9]{2,1,0:T(1,128)S(1)} all-gather(s32[1,1,9]{2,1,0:T(1,128)S(1)} %bitcast.123), channel_id=1, replica_groups=mesh['fsdp'=4,'tp'=8] {'fsdp'}, dimensions={0}, use_global_device_ids=true | all-gather | bytes 180 | tf_op jit(solution)/shard_map/all_gather | solution.py:56
  79.2 2.1 constant_dynamic-slice_fusion.1
  81.3 2.9 copy.73
  85.1 2.5 fusion.29
  87.7 34.9 %all-to-all-done.2 = bf16[128,8,1536]{0,2,1:T(8,128)(2,1)} async-done(((bf16[128,8,1536]{0,2,1:T(8,128)(2,1)}), bf16[128,8,1536]{0,2,1:T(8,128)(2,1)}, u32[]{:S(2)}, u32[]{:S(2)}) %all-to-all-start.2) | async-done | bytes 3145760 | tf_op jit(solution)/shard_map/all_to_all | solution.py:26
  122.6 3.9 fusion.7
  126.6 12.5 %fusion.10 = bf16[1536,1024]{1,0:T(8,128)(2,1)S(1)} fusion(bf16[3072,1024]{1,0:T(8,128)(2,1)} %all-gather.4.cloned.1.call-done, s32[1536]{0:T(1024)S(1)} %fusion.27), kind=kOutput, calls=%fused_computation.20 | convolution fusion | flops 9669967872 | bytes 9443328 | tf_op jit(solution)/shard_map/dot_general | solution.py:66
  139.1 1.6 copy-done.8
  140.8 6.9 %convolution_convert_fusion.1 = bf16[1536,1536]{1,0:T(8,128)(2,1)} fusion(bf16[1536,1024]{1,0:T(8,128)(2,1)S(1)} %fusion.10, bf16[1024,1536]{0,1:T(8,128)(2,1)S(1)} %fusion.7), kind=kOutput, calls=%fused_computation.7 | convolution fusion | flops 4834197504 | bytes 11010048 | tf_op jit(solution)/shard_map/dot_general | solution.py:72
  149.1 3.4 all-to-all-start.5
  152.5 2.8 copy.64
  155.3 2.1 all-to-all-done.5
  157.4 4.5 all-to-all-start.4
  162.2 2.1 constant_dynamic-slice_fusion
  164.3 2.9 copy.74
  167.2 32.5 %all-to-all-done.4 = bf16[128,8,1536]{0,2,1:T(8,128)(2,1)} async-done(((bf16[128,8,1536]{0,2,1:T(8,128)(2,1)}), bf16[128,8,1536]{0,2,1:T(8,128)(2,1)}, u32[]{:S(2)}, u32[]{:S(2)}) %all-to-all-start.4) | async-done | bytes 3145760 | tf_op jit(solution)/shard_map/all_to_all | solution.py:26
  199.8 4.0 fusion.5
  203.8 6.9 %convolution_convert_fusion = bf16[1536,1536]{1,0:T(8,128)(2,1)} fusion(bf16[1536,1024]{1,0:T(8,128)(2,1)S(1)} %copy-done.9, bf16[1024,1536]{0,1:T(8,128)(2,1)S(1)} %fusion.5), kind=kOutput, calls=%fused_computation.6 | convolution fusion | flops 4834197504 | bytes 11010048 | tf_op jit(solution)/shard_map/dot_general | solution.py:73
  211.5 7.4 %all_to_all.136 = f32[8,12,128]{2,1,0:T(8,128)S(1)} all-to-all(f32[8,12,128]{2,1,0:T(8,128)S(1)} %all_to_all.119), channel_id=1, replica_groups=mesh['fsdp'=4,'tp'=8] {'tp'}, dimensions={0} | all-to-all | bytes 98304 | tf_op jit(solution)/shard_map/all_to_all | solution.py:30
  218.9 3.7 all-to-all-start.6
  222.7 37.7 %all-to-all-done.6 = bf16[8,1536,128]{2,1,0:T(8,128)(2,1)S(1)} async-done(((bf16[8,1536,128]{2,1,0:T(8,128)(2,1)}), bf16[8,1536,128]{2,1,0:T(8,128)(2,1)S(1)}, u32[]{:S(2)}, u32[]{:S(2)}) %all-to-all-start.6) | async-done | bytes 3145760 | tf_op jit(solution)/shard_map/all_to_all | solution.py:30
  260.3 2.1 copy_bitcast_fusion
  262.5 58.8 %reduce-scatter.8.cloned.1.call-done = bf16[384,1536]{1,0:T(8,128)(2,1)} async-done(((bf16[1536,1536]{1,0:T(8,128)(2,1)}), bf16[384,1536]{1,0:T(8,128)(2,1)}) %reduce-scatter.8.cloned.1.call-update) | async-done | bytes 1179664 | tf_op jit(solution)/shard_map/reduce_scatter | solution.py:76
  321.3 3.4 fusion.16
  324.8 5.1 fusion.9
  329.9 84.9 %all-gather.6.cloned.1.call-done = bf16[1536,1536]{1,0:T(8,128)(2,1)} async-done(((bf16[384,1536]{1,0:T(8,128)(2,1)}), bf16[1536,1536]{1,0:T(8,128)(2,1)}) %all-gather.6.cloned.1.call-update) | async-done | bytes 4718608 | tf_op jit(solution)/shard_map/all_gather | solution.py:81
  414.8 8.1 %convolution_convert_fusion.2 = bf16[1536,1024]{1,0:T(8,128)(2,1)S(1)} fusion(bf16[1536,1536]{1,0:T(8,128)(2,1)} %all-gather.6.cloned.1.call-done, bf16[1536,1024]{1,0:T(8,128)(2,1)} %fusion.9), kind=kOutput, calls=%fused_computation.19 | convolution fusion | flops 4833411072 | bytes 11010048 | tf_op jit(solution)/shard_map/dot_general | solution.py:85
  422.9 3.0 copy.71
  426.0 44.5 %reduce-scatter.10.cloned.1.call-done = bf16[128,1536]{1,0:T(8,128)(2,1)} async-done(((bf16[1024,1536]{1,0:T(8,128)(2,1)}), bf16[128,1536]{1,0:T(8,128)(2,1)}) %reduce-scatter.10.cloned.1.call-update) | async-done | bytes 393232
  470.5 5.5 %fusion.11 = bf16[3008,128]{1,0:T(8,128)(2,1)} fusion(s32[3008]{0:T(1024)S(1)} %select_n.86, bf16[128,1536]{1,0:T(8,128)(2,1)} %reduce-scatter.10.cloned.1.call-done), kind=kOutput, calls=%fused_computation.21 | convolution fusion | flops 1187799040 | bytes 1175296 | tf_op jit(solution)/shard_map/dot_general | solution.py:93
  476.0 4.7 all-to-all-start.8
  480.9 19.5 %all-to-all-done.8 = bf16[4,752,128]{2,1,0:T(8,128)(2,1)S(1)} async-done(((bf16[4,752,128]{2,1,0:T(8,128)(2,1)}), bf16[4,752,128]{2,1,0:T(8,128)(2,1)S(1)}, u32[]{:S(2)}, u32[]{:S(2)}) %all-to-all-start.8) | async-done | bytes 770080 | tf_op jit(solution)/shard_map/all_to_all | solution.py:94
  500.4 1.3 bitcast_select_fusion
  501.7 3.6 all-to-all-start.9
  505.3 1.2 copy.56
  507.8 18.0 %all-to-all-done.9 = bf16[8,752,128]{2,1,0:T(8,128)(2,1)S(1)} async-done(((bf16[8,752,128]{2,1,0:T(8,128)(2,1)}), bf16[8,752,128]{2,1,0:T(8,128)(2,1)S(1)}, u32[]{:S(2)}, u32[]{:S(2)}) %all-to-all-start.9) | async-done | bytes 1540128 | tf_op jit(solution)/shard_map/all_to_all | solution.py:100
  526.4 1.4 fusion.19
  527.9 1.2 copy.70
  (69 shorter events, 10.1 us)
Async XLA Ops:
  9.3 17.8 %all-to-all-start = ((bf16[8,96,512]{2,1,0:T(8,128)(2,1)}), bf16[8,96,512]{2,1,0:T(8,128)(2,1)S(1)}, u32[]{:S(2)}, u32[]{:S(2)}) async-start(bf16[8,96,512]{2,1,0:T(8,128)(2,1)} %bitcast.7), calls=%async_computation | async-start | bytes 1572864 | tf_op jit(solution)/shard_map/all_to_all | solution.py:49
  14.5 112.1 %all-gather.4.cloned.1.call-start = ((), (), s32[]{:S(2)}) async-start(), calls=%async_computation.13 | async-start | bytes 7077888 | tf_op jit(solution)/shard_map/all_gather | solution.py:54
  30.3 24.4 %copy-start.4 = (f32[128,96]{0,1:T(8,128)S(1)}, f32[128,96]{0,1:T(8,128)}, u32[]{:S(2)}) copy-start(f32[128,96]{0,1:T(8,128)} %param.19) | copy-start | bytes 147460
  30.4 29.8 %copy-start.1 = (bf16[128,12288]{1,0:T(8,128)(2,1)S(1)}, bf16[128,12288]{1,0:T(8,128)(2,1)}, u32[]{:S(2)}) copy-start(bf16[128,12288]{1,0:T(8,128)(2,1)} %param.17) | copy-start | bytes 9437188
  55.4 9.8 %all-to-all-start.3 = ((f32[128,8,12]{0,2,1:T(8,128)}), f32[128,8,12]{0,2,1:T(8,128)S(1)}, u32[]{:S(2)}, u32[]{:S(2)}) async-start(f32[128,8,12]{0,2,1:T(8,128)} %all_to_all.107), calls=%async_computation.3 | async-start | bytes 131072 | tf_op jit(solution)/shard_map/all_to_all | solution.py:26
  65.2 4.7 copy-start.7
  65.2 57.4 %all-to-all-start.2 = ((bf16[128,8,1536]{0,2,1:T(8,128)(2,1)}), bf16[128,8,1536]{0,2,1:T(8,128)(2,1)}, u32[]{:S(2)}, u32[]{:S(2)}) async-start(bf16[128,8,1536]{0,2,1:T(8,128)(2,1)} %bitcast.11), calls=%async_computation.2 | async-start | bytes 6291456 | tf_op jit(solution)/shard_map/all_to_all | solution.py:26
  69.8 192.6 %reduce-scatter.6.cloned.1.call-start = ((), (), s32[]{:S(2)}) async-start(), calls=%async_computation.14 | async-start | bytes 5898240 | tf_op jit(solution)/shard_map/reduce_scatter | solution.py:75
  139.1 1.6 copy-start.8
  147.7 0.8 copy-start.5
  147.7 4.8 copy-start.2
  149.1 8.3 %all-to-all-start.5 = ((f32[128,8,12]{0,2,1:T(8,128)}), f32[128,8,12]{0,2,1:T(8,128)S(1)}, u32[]{:S(2)}, u32[]{:S(2)}) async-start(f32[128,8,12]{0,2,1:T(8,128)} %all_to_all.112), calls=%async_computation.6 | async-start | bytes 131072 | tf_op jit(solution)/shard_map/all_to_all | solution.py:26
  157.4 42.4 %all-to-all-start.4 = ((bf16[128,8,1536]{0,2,1:T(8,128)(2,1)}), bf16[128,8,1536]{0,2,1:T(8,128)(2,1)}, u32[]{:S(2)}, u32[]{:S(2)}) async-start(bf16[128,8,1536]{0,2,1:T(8,128)(2,1)} %bitcast.15), calls=%async_computation.5 | async-start | bytes 6291456 | tf_op jit(solution)/shard_map/all_to_all | solution.py:26
  161.9 159.4 %reduce-scatter.8.cloned.1.call-start = ((), (), s32[]{:S(2)}) async-start(), calls=%async_computation.15 | async-start | bytes 5898240 | tf_op jit(solution)/shard_map/reduce_scatter | solution.py:76
  199.8 4.0 copy-start.9
  210.7 0.8 copy-start.6
  218.9 41.4 %all-to-all-start.6 = ((bf16[8,1536,128]{2,1,0:T(8,128)(2,1)}), bf16[8,1536,128]{2,1,0:T(8,128)(2,1)S(1)}, u32[]{:S(2)}, u32[]{:S(2)}) async-start(bf16[8,1536,128]{2,1,0:T(8,128)(2,1)} %bitcast.108), calls=%async_computation.8 | async-start | bytes 6291456 | tf_op jit(solution)/shard_map/all_to_all | solution.py:30
  222.5 192.2 %all-gather.6.cloned.1.call-start = ((), (), s32[]{:S(2)}) async-start(), calls=%async_computation.16 | async-start | bytes 5898240 | tf_op jit(solution)/shard_map/all_gather | solution.py:81
  262.4 62.3 %copy-start = (bf16[1536,1024]{1,0:T(8,128)(2,1)S(1)}, bf16[1536,1024]{1,0:T(8,128)(2,1)}, u32[]{:S(2)}) copy-start(bf16[1536,1024]{1,0:T(8,128)(2,1)} %copy_bitcast_fusion) | copy-start | bytes 9437188
  324.7 145.8 %reduce-scatter.10.cloned.1.call-start = ((), (), s32[]{:S(2)}) async-start(), calls=%async_computation.17 | async-start | bytes 3538944
  476.0 29.2 %copy-start.3 = (bf16[752,512]{1,0:T(8,128)(2,1)S(1)}, bf16[752,512]{1,0:T(8,128)(2,1)}, u32[]{:S(2)}) copy-start(bf16[752,512]{1,0:T(8,128)(2,1)} %param.12) | copy-start | bytes 2310148
  476.0 24.3 %all-to-all-start.8 = ((bf16[4,752,128]{2,1,0:T(8,128)(2,1)}), bf16[4,752,128]{2,1,0:T(8,128)(2,1)S(1)}, u32[]{:S(2)}, u32[]{:S(2)}) async-start(bf16[4,752,128]{2,1,0:T(8,128)(2,1)} %bitcast.23), calls=%async_computation.10 | async-start | bytes 1540096 | tf_op jit(solution)/shard_map/all_to_all | solution.py:94
  501.7 24.2 %all-to-all-start.9 = ((bf16[8,752,128]{2,1,0:T(8,128)(2,1)}), bf16[8,752,128]{2,1,0:T(8,128)(2,1)S(1)}, u32[]{:S(2)}, u32[]{:S(2)}) async-start(bf16[8,752,128]{2,1,0:T(8,128)(2,1)} %bitcast_select_fusion), calls=%async_computation.11 | async-start | bytes 3080192 | tf_op jit(solution)/shard_map/all_to_all | solution.py:100
Sparse Core Ops, SparseCore 0:
  54.9 71.6 all-gather.3
  147.8 85.2 reduce-scatter.5
  235.4 85.7 reduce-scatter.7
  324.8 89.8 all-gather.5
  426.0 44.4 reduce-scatter.9
